TPU v7x, 32 devices: a whole 2x2x4 slice. The times are simulated.
32 devices in a mesh: dp: 8 (over z, x), blk: 4 (over y, core).
Axes of the slice: x: 2, y: 2, z: 4, core: 2. Of those that a mesh axis runs over, the one named last changes fastest.
Arguments:
- queries: bfloat16 [8, 512, 2048], P('dp', 'blk'), may hold values from -6 to 6
- keys: bfloat16 [8, 512, 512], P('dp', 'blk'), may hold values from -6 to 6
- values: bfloat16 [8, 512, 512], P('dp', 'blk'), may hold values from -6 to 6
- out_grad: bfloat16 [8, 512, 2048], P('dp', 'blk'), may hold values from -6 to 6
- layer_input: bfloat16 [8, 512, 4096], P('dp', 'blk'), may hold values from -6 to 6
- lengths: int32 [8, 3], P('dp'), may hold values from 32 to 448, as said below
Outputs:
- query_grad: bfloat16 [8, 512, 2048], P('dp', 'blk')
- key_grad: bfloat16 [8, 512, 512], P('dp', 'blk')
- value_grad: bfloat16 [8, 512, 512], P('dp', 'blk')
- weight_grad: float32 [4096, 1024], P(('dp', 'blk'))
Inputs may be any that keep to these rules, and one draw needn't show every extreme that they name: `lengths`: each row sums to 512; the chosen and rejected counts lie between 32 and 96.
All inputs are finite; a program needn't handle non-finite values.
Results may differ from a plain program's by a relative error of at most 0.023.
Values may be sent and summed in bfloat16 or wider, within the bound.
A program may use at most 128 MiB of HBM per device.

v0:
```python
import math
import jax
import jax.numpy as jnp
from jax import lax
from jax.sharding import PartitionSpec as P

HEAD = 128
rope_base = 500000.0
masked_fill = -1e30


def stored_positions(stored_rows, shard_rows, shard_count):
    half_rows = shard_rows // 2
    block_number = stored_rows // half_rows
    holder = block_number // 2
    upper_half = block_number % 2
    position_block = jnp.where(upper_half == 1, 2 * shard_count - 1 - holder, holder)
    return (position_block * half_rows + stored_rows % half_rows).astype(jnp.int32)


def allowed_pairs(query_pos, key_pos, prompt_len, chosen_len):
    causal = key_pos[None, :] <= query_pos[:, None]
    reject_start = prompt_len + chosen_len
    query_rejected = query_pos >= reject_start
    key_chosen = jnp.logical_and(key_pos >= prompt_len, key_pos < reject_start)
    return jnp.logical_and(
        causal, jnp.logical_not(jnp.logical_and(query_rejected[:, None], key_chosen[None, :]))
    )


def block_length(total_rows):
    chosen_size = 1
    for candidate in range(1, min(total_rows, 512) + 1):
        if total_rows % candidate == 0:
            chosen_size = candidate
    return chosen_size


def over_blocks(running, pieces, first_row, block_fn):
    total_rows = pieces[0].shape[0]
    block_rows = block_length(total_rows)

    def one_turn(turn_index, current):
        block_start = turn_index * block_rows
        block_parts = tuple(
            (lax.dynamic_slice_in_dim(member, block_start, block_rows, 0) for member in pieces)
        )
        return block_fn(current, block_parts, first_row + block_start)

    return lax.fori_loop(0, total_rows // block_rows, one_turn, running)


def body(queries, keys, values, out_grad, layer_input, lengths):
    shard_count = lax.axis_size("blk")
    shard_index = lax.axis_index("blk")
    shard_rows = queries.shape[1]
    kv_heads = keys.shape[2] // HEAD
    group_heads = queries.shape[2] // keys.shape[2]
    seq_len = shard_rows * shard_count
    query_count = group_heads * shard_rows
    scale = 1.0 / math.sqrt(HEAD)
    prompt_len = lengths[0, 0]
    chosen_len = lengths[0, 1]
    own_rows = shard_index * shard_rows + jnp.arange(shard_rows, dtype=jnp.int32)
    own_pos = stored_positions(own_rows, shard_rows, shard_count)
    query_pos = jnp.tile(own_pos, group_heads)
    query_rows = (
        queries[0]
        .reshape(shard_rows, kv_heads, group_heads, HEAD)
        .transpose(1, 2, 0, 3)
        .reshape(kv_heads, query_count, HEAD)
    )
    grad_rows = (
        out_grad[0]
        .reshape(shard_rows, kv_heads, group_heads, HEAD)
        .transpose(1, 2, 0, 3)
        .reshape(kv_heads, query_count, HEAD)
    )

    def block_allowed(first_row, count_rows):
        key_pos = stored_positions(
            first_row + jnp.arange(count_rows, dtype=jnp.int32), shard_rows, shard_count
        )
        return allowed_pairs(query_pos, key_pos, prompt_len, chosen_len)

    def forward_block(running, block_parts, first_row):
        key_block, value_block = block_parts
        count_rows = key_block.shape[0]
        allowed = block_allowed(first_row, count_rows)
        run_max, run_sum, run_acc = running
        key_heads = key_block.reshape(count_rows, kv_heads, HEAD)
        value_heads = value_block.reshape(count_rows, kv_heads, HEAD).astype(jnp.float32)
        scores = scale * jnp.einsum(
            "gqe,kge->gqk", query_rows, key_heads, preferred_element_type=jnp.float32
        )
        new_max = jnp.maximum(
            run_max, jnp.max(jnp.where(allowed[None], scores, masked_fill), axis=-1)
        )
        weights = jnp.where(allowed[None], jnp.exp(scores - new_max[..., None]), 0.0)
        factor = jnp.exp(run_max - new_max)
        new_sum = run_sum * factor + jnp.sum(weights, axis=-1)
        new_acc = run_acc * factor[..., None] + jnp.einsum(
            "gqk,kge->gqe", weights, value_heads, precision=lax.Precision.HIGHEST
        )
        return (new_max, new_sum, new_acc)

    start_forward = (
        jnp.full((kv_heads, query_count), masked_fill, jnp.float32),
        jnp.zeros((kv_heads, query_count), jnp.float32),
        jnp.zeros((kv_heads, query_count, HEAD), jnp.float32),
    )
    run_max, run_sum, run_acc = over_blocks(
        start_forward,
        (
            lax.all_gather(keys[0], "blk", axis=0, tiled=True),
            lax.all_gather(values[0], "blk", axis=0, tiled=True),
        ),
        jnp.int32(0),
        forward_block,
    )
    attn_out = run_acc / run_sum[..., None]
    log_total = run_max + jnp.log(run_sum)
    delta = jnp.sum(grad_rows.astype(jnp.float32) * attn_out, axis=-1)

    def backward_block(running, block_parts, first_row):
        key_block, value_block = block_parts
        count_rows = key_block.shape[0]
        allowed = block_allowed(first_row, count_rows)
        query_acc, key_acc, value_acc = running
        key_heads = key_block.reshape(count_rows, kv_heads, HEAD)
        value_heads = value_block.reshape(count_rows, kv_heads, HEAD)
        scores = scale * jnp.einsum(
            "gqe,kge->gqk", query_rows, key_heads, preferred_element_type=jnp.float32
        )
        probs = jnp.where(allowed[None], jnp.exp(scores - log_total[..., None]), 0.0)
        prob_half = probs.astype(jnp.bfloat16)
        prob_grad = jnp.einsum(
            "gqe,kge->gqk", grad_rows, value_heads, preferred_element_type=jnp.float32
        )
        score_grad = (scale * probs * (prob_grad - delta[..., None])).astype(jnp.bfloat16)
        query_acc = query_acc + jnp.einsum(
            "gqk,kge->gqe", score_grad, key_heads, preferred_element_type=jnp.float32
        )
        key_term = jnp.einsum(
            "gqk,gqe->kge", score_grad, query_rows, preferred_element_type=jnp.float32
        ).reshape(count_rows, kv_heads * HEAD)
        value_term = jnp.einsum(
            "gqk,gqe->kge", prob_half, grad_rows, preferred_element_type=jnp.float32
        ).reshape(count_rows, kv_heads * HEAD)
        key_acc = lax.dynamic_update_slice_in_dim(
            key_acc,
            lax.dynamic_slice_in_dim(key_acc, first_row, count_rows, 0) + key_term,
            first_row,
            0,
        )
        value_acc = lax.dynamic_update_slice_in_dim(
            value_acc,
            lax.dynamic_slice_in_dim(value_acc, first_row, count_rows, 0) + value_term,
            first_row,
            0,
        )
        return (query_acc, key_acc, value_acc)

    start_backward = (
        jnp.zeros((kv_heads, query_count, HEAD), jnp.float32),
        jnp.zeros((seq_len, kv_heads * HEAD), jnp.float32),
        jnp.zeros((seq_len, kv_heads * HEAD), jnp.float32),
    )
    query_acc, key_acc, value_acc = over_blocks(
        start_backward,
        (
            lax.all_gather(keys[0], "blk", axis=0, tiled=True),
            lax.all_gather(values[0], "blk", axis=0, tiled=True),
        ),
        jnp.int32(0),
        backward_block,
    )
    key_sum, value_sum = (
        lax.psum_scatter(
            key_acc.astype(jnp.bfloat16), "blk", scatter_dimension=0, tiled=True
        ).astype(jnp.float32),
        lax.psum_scatter(
            value_acc.astype(jnp.bfloat16), "blk", scatter_dimension=0, tiled=True
        ).astype(jnp.float32),
    )
    query_grad = (
        query_acc.reshape(kv_heads, group_heads, shard_rows, HEAD)
        .transpose(2, 0, 1, 3)
        .reshape(shard_rows, kv_heads * group_heads * HEAD)
        .astype(jnp.bfloat16)
    )
    key_out = key_sum.astype(jnp.bfloat16)
    value_out = value_sum.astype(jnp.bfloat16)
    half_dim = HEAD // 2
    frequency = jnp.exp(
        -(2.0 * jnp.arange(half_dim, dtype=jnp.float32) / HEAD) * math.log(rope_base)
    )
    angles = own_pos.astype(jnp.float32)[:, None] * frequency[None, :]
    cosine = jnp.concatenate([jnp.cos(angles), jnp.cos(angles)], axis=-1)[:, None, :]
    sine = jnp.concatenate([jnp.sin(angles), jnp.sin(angles)], axis=-1)[:, None, :]
    grad_heads = key_sum.reshape(shard_rows, kv_heads, HEAD)
    rotated = jnp.concatenate([-grad_heads[..., half_dim:], grad_heads[..., :half_dim]], axis=-1)
    key_pre = (
        (grad_heads * cosine - rotated * sine)
        .reshape(shard_rows, kv_heads * HEAD)
        .astype(jnp.bfloat16)
    )
    grad_cols = jnp.concatenate([key_pre, value_out], axis=1)
    input_rows = layer_input[0]
    features = layer_input.shape[2]
    replica_count = lax.axis_size("dp")
    feature_share = features // (replica_count * shard_count)
    grouped_input = input_rows.reshape(shard_rows, replica_count, shard_count * feature_share)
    sequence_input = lax.all_to_all(grouped_input, "blk", split_axis=2, concat_axis=0, tiled=True)
    sequence_weight = jnp.einsum(
        "tif,tc->ifc",
        sequence_input,
        lax.all_gather(grad_cols, "blk", axis=0, tiled=True),
        preferred_element_type=jnp.float32,
    )
    weight_grad = (
        lax.psum_scatter(
            sequence_weight.astype(jnp.bfloat16), "dp", scatter_dimension=0, tiled=True
        )
        .astype(jnp.float32)
        .reshape(feature_share, grad_cols.shape[1])
    )
    return (query_grad[None], key_out[None], value_out[None], weight_grad)


def solution(mesh):
    placed = (
        P("dp", "blk", None),
        P("dp", "blk", None),
        P("dp", "blk", None),
        P("dp", "blk", None),
        P("dp", "blk", None),
        P("dp", None),
    )
    return jax.shard_map(
        body,
        mesh=mesh,
        in_specs=placed,
        out_specs=(
            P("dp", "blk", None),
            P("dp", "blk", None),
            P("dp", "blk", None),
            P(("dp", "blk"), None),
        ),
        check_vma=False,
    )
```

profile of v0, /device:TPU:0, one launch (start us, length us, event | category | flops | bytes accessed | tf_op | source)
XLA Modules:
  0.0 209.5 jit_solution(16172209524626766928)
XLA Ops:
  7.2 1.3 fusion.41
  10.6 1.4 reshape_squeeze.9
  12.8 1.0 copy.86
  13.8 8.7 %all-gather = bf16[1,512,512]{1,2,0:T(8,128)(2,1)S(1)} all-gather(bf16[1,128,512]{1,2,0:T(8,128)(2,1)S(1)} %copy.86), channel_id=2, replica_groups=mesh['dp'=8,'blk'=4] {'blk'}, dimensions={1}, use_global_device_ids=true | all-gather | bytes 655360 | tf_op jit(solution)/shard_map/all_gather | solution.py:172
  23.8 1.9 copy-done
  28.0 7.3 %all-gather.1 = bf16[1,512,512]{1,2,0:T(8,128)(2,1)S(1)} all-gather(bf16[1,128,512]{1,2,0:T(8,128)(2,1)S(1)} %copy.90), channel_id=3, replica_groups=mesh['dp'=8,'blk'=4] {'blk'}, dimensions={1}, use_global_device_ids=true | all-gather | bytes 655360 | tf_op jit(solution)/shard_map/all_gather | solution.py:173
  35.3 4.9 %multiply_reduce_fusion = f32[4,512]{1,0:T(4,128)S(1)} fusion(bf16[4,512,128]{1,2,0:T(8,128)(2,1)S(1)} %reshape.333, bf16[512,4,128]{0,2,1:T(8,128)(2,1)S(1)} %bitcast.73, f32[4,512,512]{1,2,0:T(8,128)} %copy-done, f32[4,512]{1,0:T(4,128)S(1)} %broadcast_maximum_fusion, pred[512,512]{0,1:T(8,128)(4,1)S(1)} %not_and_fusion, ...), kind=kOutput, calls=%fused_computation.22 | convolution fusion | flops 1615067136 | bytes 5537792 | tf_op jit(solution)/shard_map/while/body/eval_jaxpr/gqk,kge->gqe/dot_general | solution.py:102
  40.2 2.7 %multiply_convert_fusion = bf16[4,512,512]{1,2,0:T(8,128)(2,1)S(1)} fusion(f32[4,512,512]{1,2,0:T(8,128)S(1)} %copy-done.1, bf16[4,512,128]{1,2,0:T(8,128)(2,1)} %copy-done.3, bf16[512,4,128]{0,2,1:T(8,128)(2,1)S(1)} %bitcast.74, f32[4,512]{1,0:T(4,128)S(1)} %multiply_reduce_fusion, f32[4,512]{1,0:T(4,128)S(1)} %get-tuple-element.90, ...), kind=kOutput, calls=%fused_computation | convolution fusion | flops 275775488 | bytes 7618560 | tf_op jit(solution)/shard_map/while/body/eval_jaxpr/gqe,kge->gqk/dot_general | solution.py:137
  42.9 1.6 convolution_convert_fusion
  44.5 2.1 copy.117
  46.6 3.4 %fusion.14 = bf16[4,512,128]{1,2,0:T(8,128)(2,1)S(1)} fusion(bf16[4,512,128]{1,2,0:T(8,128)(2,1)} %copy-done.3, f32[4,512,512]{1,2,0:T(8,128)} %copy-done, f32[4,512]{1,0:T(4,128)S(1)} %get-tuple-element.90, pred[512,512]{0,1:T(8,128)(4,1)S(1)} %not_and_fusion), kind=kOutput, calls=%fused_computation.20 | convolution fusion | flops 272891904 | bytes 5513216 | tf_op jit(solution)/shard_map/while/body/eval_jaxpr/gqk,gqe->kge/dot_general | solution.py:147
  50.0 1.0 copy.119
  51.3 18.0 %reduce-scatter.10.cloned.1.call-done = bf16[128,512]{1,0:T(8,128)(2,1)} async-done(((bf16[512,512]{1,0:T(8,128)(2,1)}), bf16[128,512]{1,0:T(8,128)(2,1)}) %reduce-scatter.10.cloned.1.call-update) | async-done | bytes 131088
  69.3 1.0 copy.118
  70.5 23.6 %reduce-scatter.12.cloned.1.call-done = bf16[128,512]{1,0:T(8,128)(2,1)} async-done(((bf16[512,512]{1,0:T(8,128)(2,1)}), bf16[128,512]{1,0:T(8,128)(2,1)}) %reduce-scatter.12.cloned.1.call-update) | async-done | bytes 131088
  94.0 1.0 copy.120
  96.0 2.3 %copy.100 = bf16[1,128,4096]{1,2,0:T(8,128)(2,1)} copy(bf16[1,128,4096]{2,1,0:T(8,128)(2,1)} %param.10) | data formatting | bytes 2097152 | tf_op args[4]
  98.3 1.9 copy.101
  100.2 22.5 %all_to_all.18 = bf16[128,8,512]{0,1,2:T(8,128)(2,1)} all-to-all(bf16[128,8,512]{0,1,2:T(8,128)(2,1)S(1)} %copy.101), channel_id=1, replica_groups=mesh['dp'=8,'blk'=4] {'blk'}, dimensions={2} | all-to-all | bytes 2097152 | tf_op jit(solution)/shard_map/all_to_all | solution.py:214
  122.8 3.0 %copy.102 = bf16[128,8,512]{2,1,0:T(8,128)(2,1)} copy(bf16[128,8,512]{0,1,2:T(8,128)(2,1)} %all_to_all.18) | data formatting | bytes 2097152 | tf_op jit(solution)/shard_map/all_to_all | solution.py:214
  125.8 2.6 %copy.103 = bf16[4,128,8,128]{3,1,0,2:T(8,128)(2,1)} copy(bf16[4,128,8,128]{3,2,0,1:T(8,128)(2,1)} %bitcast.62) | data formatting | bytes 2097152 | tf_op jit(solution)/shard_map/all_to_all | solution.py:214
  128.4 4.1 %convert_bitcast_fusion = bf16[8,128,1024]{1,2,0:T(8,128)(2,1)} fusion(bf16[512,8,128]{2,0,1:T(8,128)(2,1)} %bitcast.72, bf16[512,1024]{0,1:T(8,128)(2,1)} %all-gather.4.cloned.1.call-done), kind=kOutput, calls=%fused_computation.8 | convolution fusion | flops 1074790400 | bytes 4194304 | tf_op jit(solution)/shard_map/tif,tc->ifc/dot_general | solution.py:215
  133.8 1.2 convert_element_type.78
  136.6 64.5 %reduce-scatter.8.cloned.1.call-done = bf16[1,128,1024]{1,2,0:T(8,128)(2,1)} async-done(((bf16[8,128,1024]{1,2,0:T(8,128)(2,1)}), bf16[1,128,1024]{1,2,0:T(8,128)(2,1)}) %reduce-scatter.8.cloned.1.call-update) | async-done | bytes 262160 | tf_op jit(solution)/shard_map/reduce_scatter | solution.py:222
  (50 shorter events, 11.3 us)
Async XLA Ops:
  7.2 62.1 %reduce-scatter.10.cloned.1.call-start = ((), (), s32[]{:S(2)}) async-start(), calls=%async_computation.6 | async-start | bytes 655360
  22.8 3.9 %copy-start.2 = (bf16[1,128,2048]{2,1,0:T(8,128)(2,1)S(1)}, bf16[1,128,2048]{2,1,0:T(8,128)(2,1)}, u32[]{:S(2)}) copy-start(bf16[1,128,2048]{2,1,0:T(8,128)(2,1)} %param.9) | copy-start | bytes 1572868
  23.8 1.9 copy-start
  23.8 4.0 %copy-start.4 = (bf16[1,128,512]{2,1,0:T(8,128)(2,1)S(1)}, bf16[1,128,512]{2,1,0:T(8,128)(2,1)}, u32[]{:S(2)}) copy-start(bf16[1,128,512]{2,1,0:T(8,128)(2,1)} %param.8) | copy-start | bytes 393220
  27.8 12.4 %copy-start.3 = (bf16[4,512,128]{1,2,0:T(8,128)(2,1)}, bf16[4,512,128]{1,2,0:T(8,128)(2,1)S(1)}, u32[]{:S(2)}) copy-start(bf16[4,512,128]{1,2,0:T(8,128)(2,1)S(1)} %reshape.333) | copy-start | bytes 1572868
  35.3 4.9 %copy-start.1 = (f32[4,512,512]{1,2,0:T(8,128)S(1)}, f32[4,512,512]{1,2,0:T(8,128)}, u32[]{:S(2)}) copy-start(f32[4,512,512]{1,2,0:T(8,128)} %copy-done) | copy-start | bytes 12582916
  46.6 47.5 %reduce-scatter.12.cloned.1.call-start = ((), (), s32[]{:S(2)}) async-start(), calls=%async_computation.7 | async-start | bytes 655360
  51.0 77.3 %all-gather.4.cloned.1.call-start = ((), (), s32[]{:S(2)}) async-start(), calls=%async_computation.4 | async-start | bytes 1310720 | tf_op jit(solution)/shard_map/all_gather | solution.py:218
  95.8 105.2 %reduce-scatter.8.cloned.1.call-start = ((), (), s32[]{:S(2)}) async-start(), calls=%async_computation.5 | async-start | bytes 2359296 | tf_op jit(solution)/shard_map/reduce_scatter | solution.py:222
Sparse Core Ops, SparseCore 0:
  46.7 22.5 reduce-scatter.9
  72.4 21.6 reduce-scatter.11
  96.2 22.0 all-gather.3
  132.6 68.3 reduce-scatter.7
where the time goes:
time: 210 us
  waiting for transfers between devices  106 us (50%)
  blocking collectives  38.5 us (18%)
  local copies, waits for them, and re-layouts  26.8 us (13%)
  matrix products  18.5 us (9%)
  between operations  15.3 us (7%)
  other arithmetic  3.97 us (2%)
    reduce_scatter x1, waiting for transfers between devices, body(): lax.psum_scatter(sequence_weight.astype(jnp.bfloat16), 'dp', scatter_dime...  64.5 us
    unnamed x6, waiting for transfers between devices  41.6 us
    all_to_all x1, blocking collectives, body(): lax.all_to_all(grouped_input, 'blk', split_axis=2, concat_axis=0, tiled=T...  22.5 us
    unnamed x20, local copies, waits for them, and re-layouts  13 us
    all_gather x1, blocking collectives, body(): lax.all_gather(keys[0], 'blk', axis=0, tiled=True)  8.68 us
    all_gather x1, blocking collectives, body(): lax.all_gather(values[0], 'blk', axis=0, tiled=True)  7.29 us
    all_to_all x2, local copies, waits for them, and re-layouts, body(): lax.all_to_all(grouped_input, 'blk', split_axis=2, concat_axis=0, tiled=T...  5.62 us
    dot_general x1, matrix products, forward_block(): jnp.einsum('gqk,kge->gqe', weights, value_heads, precision=lax.Precision....  4.93 us
  transfers between devices with their start and end apart: 4, of which 3 were waited for; matrix products, arithmetic and copies ran while one was open for 9% of the time, Pallas kernels for 0%

commit v1 on v0

--- a/solution.py
+++ b/solution.py
@@ -211,7 +211,9 @@
     replica_count = lax.axis_size("dp")
     feature_share = features // (replica_count * shard_count)
     grouped_input = input_rows.reshape(shard_rows, replica_count, shard_count * feature_share)
-    sequence_input = lax.all_to_all(grouped_input, "blk", split_axis=2, concat_axis=0, tiled=True)
+    parts = jnp.split(grouped_input, lax.axis_size("blk"), axis=2)
+    got = lax.all_to_all(jnp.stack(parts), "blk", 0, 0)
+    sequence_input = jnp.concatenate(got, axis=0)
     sequence_weight = jnp.einsum(
         "tif,tc->ifc",
         sequence_input,

time: 210 us -> 203 us (0.967)
  local copies, waits for them, and re-layouts: 26.8 us -> 15.2 us
  other arithmetic: 3.97 us -> 7.34 us
    unnamed x6 -> x4, waiting for transfers between devices: 41.6 us -> 0.07 us
    reduce_scatter x0 -> x2, waiting for transfers between devices: none -> 40 us  [the longest x1 22.3 us: body(): lax.psum_scatter(value_acc.astype(jnp.bfloat16), 'blk', scatter_dimension...]
    unnamed x20 -> x13, local copies, waits for them, and re-layouts: 13 us -> 4.7 us
    all_to_all x2 -> x0, local copies, waits for them, and re-layouts: 5.62 us -> none  [body(): lax.all_to_all(grouped_input, 'blk', split_axis=2, concat_axis=0, tiled=T...]
    convert_element_type x0 -> x2, local copies, waits for them, and re-layouts: none -> 3.06 us  [the longest x1 2.05 us: body(): key_acc.astype(jnp.bfloat16)]
  transfers between devices with their start and end apart: 4 -> 4, of which waited for: 3 -> 3; matrix products, arithmetic and copies ran while one was open for 9% -> 6% of each run, Pallas kernels for 0% -> 0%
where the time goes in v1:
time: 203 us; the launch traced here: 202 us
  waiting for transfers between devices  106 us (52%)
  blocking collectives  39.2 us (19%)
  matrix products  18.6 us (9%)
  between operations  15.3 us (8%)
  local copies, waits for them, and re-layouts  15.2 us (7%)
  other arithmetic  7.34 us (4%)
    reduce_scatter x1, waiting for transfers between devices, body(): lax.psum_scatter(sequence_weight.astype(jnp.bfloat16), 'dp', scatter_dime...  66.1 us
    all_to_all x1, blocking collectives, body(): got = lax.all_to_all(jnp.stack(parts), 'blk', 0, 0)  23.2 us
    reduce_scatter x1, waiting for transfers between devices, body(): lax.psum_scatter(value_acc.astype(jnp.bfloat16), 'blk', scatter_dimension...  22.3 us
    reduce_scatter x1, waiting for transfers between devices, body(): lax.psum_scatter(key_acc.astype(jnp.bfloat16), 'blk', scatter_dimension=0...  17.7 us
    all_gather x1, blocking collectives, body(): lax.all_gather(keys[0], 'blk', axis=0, tiled=True)  8.68 us
    all_gather x1, blocking collectives, body(): lax.all_gather(values[0], 'blk', axis=0, tiled=True)  7.29 us
    dot_general x1, matrix products, forward_block(): jnp.einsum('gqk,kge->gqe', weights, value_heads, precision=lax.Precision....  4.93 us
    unnamed x13, local copies, waits for them, and re-layouts  4.7 us
  transfers between devices with their start and end apart: 4, of which 3 were waited for; matrix products, arithmetic and copies ran while one was open for 6% of the time, Pallas kernels for 0%

profile of v1, /device:TPU:0, one launch (start us, length us, event | category | flops | bytes accessed | tf_op | source)
XLA Modules:
  0.0 202.2 jit_solution(17738924869191291380)
XLA Ops:
  7.2 1.3 fusion.42
  10.6 1.4 reshape_squeeze.9
  12.8 1.0 copy.28
  13.8 8.7 %all-gather = bf16[1,512,512]{1,2,0:T(8,128)(2,1)S(1)} all-gather(bf16[1,128,512]{1,2,0:T(8,128)(2,1)S(1)} %copy.28), channel_id=2, replica_groups=mesh['dp'=8,'blk'=4] {'blk'}, dimensions={1}, use_global_device_ids=true | all-gather | bytes 655360 | tf_op jit(solution)/shard_map/all_gather | solution.py:172
  22.8 1.0 select_reduce_fusion
  23.8 1.9 copy-done
  28.0 7.3 %all-gather.1 = bf16[1,512,512]{1,2,0:T(8,128)(2,1)S(1)} all-gather(bf16[1,128,512]{1,2,0:T(8,128)(2,1)S(1)} %copy.32), channel_id=3, replica_groups=mesh['dp'=8,'blk'=4] {'blk'}, dimensions={1}, use_global_device_ids=true | all-gather | bytes 655360 | tf_op jit(solution)/shard_map/all_gather | solution.py:173
  35.3 4.9 %multiply_reduce_fusion = f32[4,512]{1,0:T(4,128)S(1)} fusion(bf16[4,512,128]{1,2,0:T(8,128)(2,1)S(1)} %reshape.336, bf16[512,4,128]{0,2,1:T(8,128)(2,1)S(1)} %bitcast.73, f32[4,512,512]{1,2,0:T(8,128)} %copy-done, f32[4,512]{1,0:T(4,128)S(1)} %broadcast_maximum_fusion, pred[512,512]{0,1:T(8,128)(4,1)S(1)} %not_and_fusion, ...), kind=kOutput, calls=%fused_computation.24 | convolution fusion | flops 1615067136 | bytes 5537792 | tf_op jit(solution)/shard_map/while/body/eval_jaxpr/gqk,kge->gqe/dot_general | solution.py:102
  40.2 2.7 %multiply_convert_fusion = bf16[4,512,512]{1,2,0:T(8,128)(2,1)S(1)} fusion(f32[4,512,512]{1,2,0:T(8,128)S(1)} %copy-done.1, bf16[4,512,128]{1,2,0:T(8,128)(2,1)} %copy-done.3, bf16[512,4,128]{0,2,1:T(8,128)(2,1)S(1)} %bitcast.74, f32[4,512]{1,0:T(4,128)S(1)} %multiply_reduce_fusion, f32[4,512]{1,0:T(4,128)S(1)} %get-tuple-element.61, ...), kind=kOutput, calls=%fused_computation | convolution fusion | flops 275775488 | bytes 7618560 | tf_op jit(solution)/shard_map/while/body/eval_jaxpr/gqe,kge->gqk/dot_general | solution.py:137
  42.9 1.6 convolution_convert_fusion.1
  44.5 2.1 %copy.41 = bf16[512,512]{1,0:T(8,128)(2,1)} copy(bf16[512,512]{0,1:T(8,128)(2,1)} %bitcast.69) | data formatting | bytes 1048576 | tf_op jit(solution)/shard_map/convert_element_type | solution.py:180
  46.6 3.4 %fusion.14 = bf16[4,512,128]{1,2,0:T(8,128)(2,1)S(1)} fusion(bf16[4,512,128]{1,2,0:T(8,128)(2,1)} %copy-done.3, f32[4,512,512]{1,2,0:T(8,128)} %copy-done, f32[4,512]{1,0:T(4,128)S(1)} %get-tuple-element.61, pred[512,512]{0,1:T(8,128)(4,1)S(1)} %not_and_fusion), kind=kOutput, calls=%fused_computation.20 | convolution fusion | flops 272891904 | bytes 5513216 | tf_op jit(solution)/shard_map/while/body/eval_jaxpr/gqk,gqe->kge/dot_general | solution.py:147
  50.0 1.0 copy.43
  51.6 17.7 %reduce-scatter.4.cloned.1.call-done = bf16[128,512]{1,0:T(8,128)(2,1)} async-done(((bf16[512,512]{1,0:T(8,128)(2,1)}), bf16[128,512]{1,0:T(8,128)(2,1)}) %reduce-scatter.4.cloned.1.call-update) | async-done | bytes 131088 | tf_op jit(solution)/shard_map/reduce_scatter | solution.py:179
  69.3 1.0 reshape.339
  70.8 1.0 fusion.19
  71.7 22.3 %reduce-scatter.6.cloned.1.call-done = bf16[128,512]{1,0:T(8,128)(2,1)} async-done(((bf16[512,512]{1,0:T(8,128)(2,1)}), bf16[128,512]{1,0:T(8,128)(2,1)}) %reduce-scatter.6.cloned.1.call-update) | async-done | bytes 131088 | tf_op jit(solution)/shard_map/reduce_scatter | solution.py:182
  94.1 1.6 pad_maximum_fusion.1
  95.9 1.6 copy.56
  97.9 23.2 %all_to_all.5 = bf16[4,128,8,128]{3,2,1,0:T(8,128)(2,1)} all-to-all(bf16[4,128,8,128]{3,2,1,0:T(8,128)(2,1)S(1)} %pad_maximum_fusion), channel_id=1, replica_groups=mesh['dp'=8,'blk'=4] {'blk'}, dimensions={0} | all-to-all | bytes 2097152 | tf_op jit(solution)/shard_map/all_to_all | solution.py:215
  121.1 4.2 %convolution_convert_fusion = bf16[8,128,1024]{2,1,0:T(8,128)(2,1)} fusion(bf16[512,1024]{1,0:T(8,128)(2,1)} %all-gather.4.cloned.1.call-done, bf16[512,8,128]{2,1,0:T(8,128)(2,1)} %bitcast.65), kind=kOutput, calls=%fused_computation.16 | convolution fusion | flops 1074790400 | bytes 4194304 | tf_op jit(solution)/shard_map/tif,tc->ifc/dot_general | solution.py:217
  126.6 1.2 convert_element_type.75
  127.8 66.1 %reduce-scatter.8.cloned.1.call-done = bf16[1,128,1024]{2,1,0:T(8,128)(2,1)} async-done(((bf16[8,128,1024]{2,1,0:T(8,128)(2,1)}), bf16[1,128,1024]{2,1,0:T(8,128)(2,1)}) %reduce-scatter.8.cloned.1.call-update) | async-done | bytes 262160 | tf_op jit(solution)/shard_map/reduce_scatter | solution.py:224
  193.9 1.8 bitcast_convert_fusion
  (44 shorter events, 7.0 us)
Async XLA Ops:
  7.2 62.1 %reduce-scatter.4.cloned.1.call-start = ((), (), s32[]{:S(2)}) async-start(), calls=%async_computation.4 | async-start | bytes 655360 | tf_op jit(solution)/shard_map/reduce_scatter | solution.py:179
  22.8 3.9 %copy-start.2 = (bf16[1,128,2048]{2,1,0:T(8,128)(2,1)S(1)}, bf16[1,128,2048]{2,1,0:T(8,128)(2,1)}, u32[]{:S(2)}) copy-start(bf16[1,128,2048]{2,1,0:T(8,128)(2,1)} %param.9) | copy-start | bytes 1572868
  23.8 1.9 copy-start
  23.8 4.1 %copy-start.4 = (bf16[1,128,512]{2,1,0:T(8,128)(2,1)S(1)}, bf16[1,128,512]{2,1,0:T(8,128)(2,1)}, u32[]{:S(2)}) copy-start(bf16[1,128,512]{2,1,0:T(8,128)(2,1)} %param.8) | copy-start | bytes 393220
  27.8 12.4 %copy-start.3 = (bf16[4,512,128]{1,2,0:T(8,128)(2,1)}, bf16[4,512,128]{1,2,0:T(8,128)(2,1)S(1)}, u32[]{:S(2)}) copy-start(bf16[4,512,128]{1,2,0:T(8,128)(2,1)S(1)} %reshape.336) | copy-start | bytes 1572868
  35.3 4.9 %copy-start.1 = (f32[4,512,512]{1,2,0:T(8,128)S(1)}, f32[4,512,512]{1,2,0:T(8,128)}, u32[]{:S(2)}) copy-start(f32[4,512,512]{1,2,0:T(8,128)} %copy-done) | copy-start | bytes 12582916
  46.6 47.5 %reduce-scatter.6.cloned.1.call-start = ((), (), s32[]{:S(2)}) async-start(), calls=%async_computation.5 | async-start | bytes 655360 | tf_op jit(solution)/shard_map/reduce_scatter | solution.py:182
  51.0 70.1 %all-gather.4.cloned.1.call-start = ((), (), s32[]{:S(2)}) async-start(), calls=%async_computation.6 | async-start | bytes 1310720 | tf_op jit(solution)/shard_map/all_gather | solution.py:220
  95.7 98.2 %reduce-scatter.8.cloned.1.call-start = ((), (), s32[]{:S(2)}) async-start(), calls=%async_computation.7 | async-start | bytes 2359296 | tf_op jit(solution)/shard_map/reduce_scatter | solution.py:224
Sparse Core Ops, SparseCore 0:
  46.7 22.5 reduce-scatter.3
  72.3 21.6 reduce-scatter.5
  96.2 22.4 all-gather.3
  125.4 68.4 reduce-scatter.7
